TPU v7x, 32 devices: a whole 2x2x4 slice. The times are simulated.
32 devices in a mesh: dp: 4 (over x, core), mp: 8 (over z, y).
Axes of the slice: x: 2, y: 2, z: 4, core: 2. Of those that a mesh axis runs over, the one named last changes fastest.
Arguments:
- tokens: bfloat16 [128, 8192], P('dp', 'mp'), may hold values from -6 to 6
- gate_up_weight: bfloat16 [2, 8192, 15360], P(None, 'mp', 'dp'), may hold values from -0.0625 to 0.0625
- down_weight: bfloat16 [15360, 8192], P('dp', 'mp'), may hold values from -0.046875 to 0.046875
- gate_up_input_factor: bfloat16 [2, 8192, 64], P(None, 'mp'), may hold values from -0.0625 to 0.0625
- gate_up_output_factor: bfloat16 [2, 64, 15360], P(None, None, 'dp'), may hold values from -0.046875 to 0.046875
- down_input_factor: bfloat16 [15360, 64], P('dp'), may hold values from -0.046875 to 0.046875
- down_output_factor: bfloat16 [64, 8192], P(None, 'mp'), may hold values from -0.0625 to 0.0625
- cotangent: bfloat16 [128, 8192], P('dp', 'mp'), may hold values from -6 to 6
Outputs:
- output: bfloat16 [128, 8192], P('dp', 'mp')
- input_grad: bfloat16 [128, 8192], P('dp', 'mp')
- grad_gate_up_lower: float32 [2, 8192, 64], P(None, 'mp')
- gate_up_output_factor_gradient: float32 [2, 64, 15360], P(None, None, 'dp')
- down_input_factor_gradient: float32 [15360, 64], P('dp')
- down_output_factor_gradient: float32 [64, 8192], P(None, 'mp')
All inputs are finite; a program needn't handle non-finite values.
Results may differ from a plain program's by a relative error of at most 0.0065.
Values may be sent and summed in bfloat16 or wider, within the bound.
A program may use at most 64 MiB of HBM per device.

v0:
```python
import jax
import jax.numpy as jnp
from jax import lax
from jax.sharding import PartitionSpec as P

adapter_scale = 2.0


def contract_trailing(left, right, matmul_precision=None):
    return lax.dot_general(
        left,
        right,
        (((1,), (1,)), ((), ())),
        preferred_element_type=jnp.float32,
        precision=matmul_precision,
    )


def contract_leading(left, right, matmul_precision=None):
    return lax.dot_general(
        left,
        right,
        (((0,), (0,)), ((), ())),
        preferred_element_type=jnp.float32,
        precision=matmul_precision,
    )


def per_device(
    tokens,
    gate_up_weight,
    down_weight,
    gate_up_input_factor,
    gate_up_output_factor,
    down_input_factor,
    down_output_factor,
    cotangent,
):
    single_float = jnp.float32
    upper_projection = lax.Precision.HIGHEST
    tok_rows = tokens.shape[0]
    input_rows_full = lax.all_gather(tokens, "dp", axis=0, tiled=True)
    total = input_rows_full.shape[0]
    mp_rows = total // lax.axis_size("mp")
    scale_factor = total ** (-0.5)
    mp_start = lax.axis_index("mp") * mp_rows
    dp_start = lax.axis_index("dp") * tok_rows
    low_part = jnp.einsum(
        "td,kdr->tkr", input_rows_full, gate_up_input_factor, preferred_element_type=single_float
    )
    upper_widened = gate_up_output_factor.astype(single_float)
    term = jnp.einsum(
        "td,kdf->tkf", input_rows_full, gate_up_weight, preferred_element_type=single_float
    )
    low_slab = low_part
    term = term + adapter_scale * jnp.einsum(
        "ubw,bwa->uba", low_slab, upper_widened, precision=upper_projection
    )
    preactivation = lax.psum_scatter(term, "mp", scatter_dimension=0, tiled=True)
    gate = preactivation[:, 0]
    upper = preactivation[:, 1]
    hidden_state = (jax.nn.silu(gate) * upper).astype(jnp.bfloat16)
    hidden_state_full = lax.all_gather(hidden_state, "mp", axis=0, tiled=True)
    low_down_part = jnp.dot(
        hidden_state_full, down_input_factor, preferred_element_type=single_float
    )
    down_widened_rows = down_output_factor.astype(single_float)
    term = jnp.dot(hidden_state_full, down_weight, preferred_element_type=single_float)
    low_slab = low_down_part
    term = term + adapter_scale * jnp.dot(low_slab, down_widened_rows, precision=upper_projection)
    output = lax.psum_scatter(term, "dp", scatter_dimension=0, tiled=True)
    output = output.astype(jnp.bfloat16)
    cot_all = lax.all_gather(cotangent, "dp", axis=0, tiled=True)
    coeff_part = contract_leading(
        low_down_part, cot_all.astype(single_float), matmul_precision=upper_projection
    )
    down_coefficient = lax.psum(coeff_part, "dp")
    backward_down_rows = lax.psum(contract_trailing(cot_all, down_output_factor), "mp").astype(
        jnp.bfloat16
    )
    hidden_state_gradient = lax.psum_scatter(
        contract_trailing(cot_all, down_weight), "mp", scatter_dimension=0, tiled=True
    )
    backward_row_block = lax.dynamic_slice_in_dim(backward_down_rows, mp_start, mp_rows, 0)
    hidden_state_gradient = hidden_state_gradient + adapter_scale * contract_trailing(
        backward_row_block, down_input_factor
    )
    down_input_factor_gradient = (
        adapter_scale * scale_factor * contract_leading(hidden_state_full, backward_down_rows)
    )
    sigma = jax.nn.sigmoid(gate)
    gate_back = hidden_state_gradient * upper * sigma * (1.0 + gate * (1.0 - sigma))
    up_back = hidden_state_gradient * gate * sigma
    pre_back = jnp.stack([gate_back, up_back], axis=1).astype(jnp.bfloat16)
    back_all = lax.all_gather(pre_back, "mp", axis=0, tiled=True)
    upper_partial = jnp.einsum(
        "tkr,tkf->krf", low_part, back_all.astype(single_float), precision=upper_projection
    )
    gate_up_output_factor_gradient = adapter_scale * scale_factor * lax.psum(upper_partial, "mp")
    back_low_part = jnp.einsum(
        "tkf,krf->tkr", back_all, gate_up_output_factor, preferred_element_type=single_float
    )
    back_low_sum = lax.psum(back_low_part, "dp")
    down_output_factor_gradient = adapter_scale * scale_factor * down_coefficient
    backward_lower_rows = back_low_sum.astype(jnp.bfloat16)
    grad_gate_up_lower = (
        adapter_scale
        * scale_factor
        * jnp.einsum(
            "qi,qps->pis", input_rows_full, backward_lower_rows, preferred_element_type=single_float
        )
    )
    input_total_sum = lax.psum_scatter(
        jnp.einsum("tkf,kdf->td", back_all, gate_up_weight, preferred_element_type=single_float),
        "dp",
        scatter_dimension=0,
        tiled=True,
    )
    low_rows_back = lax.dynamic_slice_in_dim(backward_lower_rows, dp_start, tok_rows, 0)
    input_total_sum = input_total_sum + adapter_scale * jnp.einsum(
        "tkr,kdr->td", low_rows_back, gate_up_input_factor, preferred_element_type=single_float
    )
    input_grad = input_total_sum.astype(jnp.bfloat16)
    return (
        output,
        input_grad,
        grad_gate_up_lower,
        gate_up_output_factor_gradient,
        down_input_factor_gradient,
        down_output_factor_gradient,
    )


def solution(mesh):
    placed = (
        P("dp", "mp"),
        P(None, "mp", "dp"),
        P("dp", "mp"),
        P(None, "mp", None),
        P(None, None, "dp"),
        P("dp", None),
        P(None, "mp"),
        P("dp", "mp"),
    )
    return jax.shard_map(
        per_device,
        mesh=mesh,
        in_specs=placed,
        out_specs=(
            P("dp", "mp"),
            P("dp", "mp"),
            P(None, "mp", None),
            P(None, None, "dp"),
            P("dp", None),
            P(None, "mp"),
        ),
        check_vma=False,
    )
```

profile of v0, /device:TPU:0, one launch (start us, length us, event | category | flops | bytes accessed | tf_op | source)
XLA Modules:
  0.0 428.3 jit_solution(14239089017707970945)
XLA Ops:
  7.2 0.0 copy-start
  7.2 0.0 reduce-scatter.9.cloned.1.call-start
  7.2 7.6 %all_gather.14 = bf16[128,1024]{1,0:T(8,128)(2,1)S(1)} all-gather(bf16[32,1024]{1,0:T(8,128)(2,1)} %param.15), channel_id=1, replica_groups=mesh['dp'=4,'mp'=8] {'dp'}, dimensions={0}, use_global_device_ids=true | all-gather | bytes 327680 | tf_op jit(solution)/shard_map/all_gather | solution.py:73
  14.8 0.0 copy-start.4
  14.8 0.0 copy-start.1
  14.8 7.2 %fusion.22 = f32[128,3840]{1,0:T(8,128)} fusion(bf16[128,1024]{1,0:T(8,128)(2,1)S(1)} %all_gather.14, bf16[3840,1024]{1,0:T(8,128)(2,1)} %param.10), kind=kOutput, calls=%fused_computation.37 | convolution fusion | flops 1006632960 | bytes 10092544 | tf_op jit(solution)/shard_map/dot_general | solution.py:10
  22.0 0.0 reduce-scatter.9.cloned.1.call-update
  22.0 0.0 reduce-scatter.5.cloned.1.call-start
  22.1 0.0 copy-done.4
  22.1 5.9 %all_gather.12 = bf16[128,1024]{1,0:T(8,128)(2,1)S(1)} all-gather(bf16[32,1024]{1,0:T(8,128)(2,1)S(1)} %copy-done.4), channel_id=1, replica_groups=mesh['dp'=4,'mp'=8] {'dp'}, dimensions={0}, use_global_device_ids=true | all-gather | bytes 327680 | tf_op jit(solution)/shard_map/all_gather | solution.py:42
  28.0 0.0 copy-done.1
  28.0 0.2 fusion.19
  28.2 7.9 %fusion.9 = f32[128,2,3840]{2,0,1:T(8,128)S(1)} fusion(bf16[2,1024,3840]{2,1,0:T(8,128)(2,1)} %param.9, bf16[128,1024]{1,0:T(8,128)(2,1)S(1)} %all_gather.12), kind=kOutput, calls=%fused_computation.18 | convolution fusion | flops 2013265920 | bytes 19922944 | tf_op jit(solution)/shard_map/td,kdf->tkf/dot_general | solution.py:52
  36.1 0.0 copy-done
  36.1 3.9 fusion.1
  40.0 0.0 copy-start.2
  40.0 0.0 copy-start.3
  40.0 0.0 reduce-scatter.5.cloned.1.call-update
  40.0 0.0 all-gather.2.cloned.1.call-start
  40.1 0.8 copy-done.2
  40.9 0.2 fusion.23
  41.1 37.6 %psum.28 = bf16[128,64]{0,1:T(8,128)(2,1)S(1)} all-reduce(f32[128,64]{0,1:T(8,128)S(1)} %fusion.23), channel_id=1, replica_groups=mesh['dp'=4,'mp'=8] {'mp'}, use_global_device_ids=true, to_apply=%region_3.4 | all-reduce | flops 8192 | bytes 49152 | tf_op jit(solution)/shard_map/psum | solution.py:78
  78.7 12.6 %reduce-scatter.9.cloned.1.call-done = f32[16,3840]{1,0:T(8,128)} async-done(((f32[128,3840]{1,0:T(8,128)}), f32[16,3840]{1,0:T(8,128)}) %reduce-scatter.9.cloned.1.call-update) | async-done | bytes 245776 | tf_op jit(solution)/shard_map/reduce_scatter | solution.py:81
  91.3 87.4 %reduce-scatter.5.cloned.1.call-done = f32[16,2,3840]{2,0,1:T(8,128)} async-done(((f32[128,2,3840]{2,0,1:T(8,128)}), f32[16,2,3840]{2,0,1:T(8,128)}) %reduce-scatter.5.cloned.1.call-update) | async-done | bytes 491536 | tf_op jit(solution)/shard_map/reduce_scatter | solution.py:59
  178.7 0.0 copy-done.3
  178.7 2.2 fusion.12
  180.9 0.7 pad_maximum_fusion
  181.6 0.0 all-gather.2.cloned.1.call-update
  181.6 0.0 all-reduce.5.cloned.1.call-start
  181.7 34.2 %all_gather.13 = bf16[128,3840]{1,0:T(8,128)(2,1)S(1)} all-gather(bf16[16,3840]{1,0:T(8,128)(2,1)} %get-tuple-element.8), channel_id=1, replica_groups=mesh['dp'=4,'mp'=8] {'mp'}, dimensions={0}, use_global_device_ids=true | all-gather | bytes 1105920 | tf_op jit(solution)/shard_map/all_gather | solution.py:63
  215.9 0.4 fusion.21
  216.3 1.0 fusion.25
  217.3 4.4 %fusion.20 = f32[128,1024]{1,0:T(8,128)S(1)} fusion(bf16[128,3840]{1,0:T(8,128)(2,1)S(1)} %all_gather.13, bf16[3840,1024]{1,0:T(8,128)(2,1)} %param.10), kind=kOutput, calls=%fused_computation.35 | convolution fusion | flops 1006632960 | bytes 9371648 | tf_op jit(solution)/shard_map/dot_general | solution.py:68
  221.8 0.0 all-reduce.5.cloned.1.call-update
  221.8 0.0 reduce-scatter.7.cloned.1.call-start
  221.8 1.2 fusion.4
  223.1 0.0 reduce-scatter.7.cloned.1.call-update
  223.1 0.0 reduce-scatter.11.cloned.1.call-start
  223.1 9.7 %all-gather.2.cloned.1.call-done = bf16[128,2,3840]{2,0,1:T(8,128)(2,1)} async-done(((bf16[16,2,3840]{2,0,1:T(8,128)(2,1)}), bf16[128,2,3840]{2,0,1:T(8,128)(2,1)}) %all-gather.2.cloned.1.call-update) | async-done | bytes 1966096 | tf_op jit(solution)/shard_map/all_gather | solution.py:95
  232.8 11.9 %convolution_bitcast_fusion = f32[128,1024]{1,0:T(8,128)} fusion(bf16[128,2,3840]{2,0,1:T(8,128)(2,1)} %all-gather.2.cloned.1.call-done, bf16[2,1024,3840]{2,1,0:T(8,128)(2,1)} %param.9), kind=kOutput, calls=%fused_computation.6 | convolution fusion | flops 2013265920 | bytes 18219008 | tf_op jit(solution)/shard_map/tkf,kdf->td/dot_general | solution.py:114
  244.8 0.0 reduce-scatter.11.cloned.1.call-update
  244.8 0.2 all-reduce.3.cloned.1.call-start
  245.0 3.8 fusion.24
  248.8 0.0 all-reduce.3.cloned.1.call-update
  248.8 1.2 convolution_multiply_fusion.1
  250.0 17.3 %all-reduce.5.cloned.1.call-done = f32[64,1024]{1,0:T(8,128)} async-done(((f32[64,1024]{1,0:T(8,128)}), f32[64,1024]{1,0:T(8,128)}) %all-reduce.5.cloned.1.call-update) | async-done | bytes 262160 | tf_op jit(solution)/shard_map/psum | solution.py:77
  267.3 1.7 broadcast_multiply_fusion.1
  269.0 22.9 %reduce-scatter.7.cloned.1.call-done = f32[32,1024]{1,0:T(8,128)} async-done(((f32[128,1024]{1,0:T(8,128)}), f32[32,1024]{1,0:T(8,128)}) %reduce-scatter.7.cloned.1.call-update) | async-done | bytes 131088 | tf_op jit(solution)/shard_map/reduce_scatter | solution.py:71
  291.9 1.5 convert_element_type.21
  293.4 2.3 convolution_bitcast_fusion.2
  295.7 10.7 %psum.29 = bf16[128,2,64]{0,2,1:T(8,128)(2,1)S(1)} all-reduce(f32[128,2,64]{0,2,1:T(8,128)S(1)} %convolution_bitcast_fusion.2), channel_id=1, replica_groups=mesh['dp'=4,'mp'=8] {'dp'}, use_global_device_ids=true, to_apply=%region_5.6 | all-reduce | flops 16384 | bytes 98304 | tf_op jit(solution)/shard_map/psum | solution.py:103
  306.4 1.0 fusion.3
  307.4 8.4 %reduce-scatter.11.cloned.1.call-done = f32[32,1024]{1,0:T(8,128)} async-done(((f32[128,1024]{1,0:T(8,128)}), f32[32,1024]{1,0:T(8,128)}) %reduce-scatter.11.cloned.1.call-update) | async-done | bytes 131088 | tf_op jit(solution)/shard_map/reduce_scatter | solution.py:113
  315.9 1.8 fusion.7
  317.7 100.8 %all-reduce.3.cloned.1.call-done = f32[2,64,3840]{2,1,0:T(8,128)} async-done(((f32[2,64,3840]{2,1,0:T(8,128)}), f32[2,64,3840]{2,1,0:T(8,128)}) %all-reduce.3.cloned.1.call-update) | async-done | bytes 1966096 | tf_op jit(solution)/shard_map/psum | solution.py:99
  418.4 3.0 broadcast_multiply_fusion
Async XLA Ops:
  7.2 28.9 %copy-start = (bf16[2,64,3840]{2,1,0:T(8,128)(2,1)S(1)}, bf16[2,64,3840]{2,1,0:T(8,128)(2,1)}, u32[]{:S(2)}) copy-start(bf16[2,64,3840]{2,1,0:T(8,128)(2,1)} %param.12) | copy-start | bytes 2949124
  7.2 84.1 %reduce-scatter.9.cloned.1.call-start = ((), (), s32[]{:S(2)}) async-start(), calls=%async_computation.6 | async-start | bytes 2211840 | tf_op jit(solution)/shard_map/reduce_scatter | solution.py:81
  14.8 7.3 %copy-start.4 = (bf16[32,1024]{1,0:T(8,128)(2,1)S(1)}, bf16[32,1024]{1,0:T(8,128)(2,1)}, u32[]{:S(2)}) copy-start(bf16[32,1024]{1,0:T(8,128)(2,1)} %param.8) | copy-start | bytes 196612
  14.8 13.2 %copy-start.1 = (bf16[2,1024,64]{1,2,0:T(8,128)(2,1)S(1)}, bf16[2,1024,64]{1,2,0:T(8,128)(2,1)}, u32[]{:S(2)}) copy-start(bf16[2,1024,64]{1,2,0:T(8,128)(2,1)} %param.11) | copy-start | bytes 786436
  22.0 156.7 %reduce-scatter.5.cloned.1.call-start = ((), (), s32[]{:S(2)}) async-start(), calls=%async_computation.4 | async-start | bytes 4423680 | tf_op jit(solution)/shard_map/reduce_scatter | solution.py:59
  40.0 0.9 copy-start.2
  40.0 138.7 %copy-start.3 = (bf16[3840,64]{0,1:T(8,128)(2,1)S(1)}, bf16[3840,64]{0,1:T(8,128)(2,1)}, u32[]{:S(2)}) copy-start(bf16[3840,64]{0,1:T(8,128)(2,1)} %param.13) | copy-start | bytes 1474564
  40.0 192.8 %all-gather.2.cloned.1.call-start = ((), (), s32[]{:S(2)}) async-start(), calls=%async_computation.7 | async-start | bytes 2211840 | tf_op jit(solution)/shard_map/all_gather | solution.py:95
  181.6 85.6 %all-reduce.5.cloned.1.call-start = ((), (), s32[]{:S(2)}) async-start(), calls=%async_computation.10 | async-start | bytes 524288 | tf_op jit(solution)/shard_map/psum | solution.py:77
  221.8 70.1 %reduce-scatter.7.cloned.1.call-start = ((), (), s32[]{:S(2)}) async-start(), calls=%async_computation.5 | async-start | bytes 655360 | tf_op jit(solution)/shard_map/reduce_scatter | solution.py:71
  223.1 92.8 %reduce-scatter.11.cloned.1.call-start = ((), (), s32[]{:S(2)}) async-start(), calls=%async_computation.8 | async-start | bytes 655360 | tf_op jit(solution)/shard_map/reduce_scatter | solution.py:113
  244.8 173.7 %all-reduce.3.cloned.1.call-start = ((), (), s32[]{:S(2)}) async-start(), calls=%async_computation.9 | async-start | bytes 3932160 | tf_op jit(solution)/shard_map/psum | solution.py:99
Sparse Core Ops, SparseCore 0:
  22.2 69.1 reduce-scatter.8
  95.0 83.6 reduce-scatter.4
  181.8 51.0 all-gather.1
  235.6 31.6 all-reduce.4
  270.2 21.6 reduce-scatter.6
  294.2 21.6 reduce-scatter.10
  320.0 98.3 all-reduce.2
where the time goes:
time: 429 us; the launch traced here: 428 us
  waiting for transfers between devices  259 us (60%)
  blocking collectives  95.9 us (22%)
  matrix products  50.8 us (12%)
  between operations  14.2 us (3%)
  other arithmetic  6.92 us (2%)
    psum x1, waiting for transfers between devices, per_device(): lax.psum(upper_partial, 'mp')  101 us
    reduce_scatter x1, waiting for transfers between devices, per_device(): lax.psum_scatter(term, 'mp', scatter_dimension=0, tiled=True)  87.4 us
    psum x1, blocking collectives, per_device(): lax.psum(contract_trailing(cot_all, down_output_factor), 'mp')  37.6 us
    all_gather x1, blocking collectives, per_device(): hidden_state_full = lax.all_gather(hidden_state, 'mp', axis=0, tiled=True)  34.2 us
    reduce_scatter x1, waiting for transfers between devices, per_device(): output = lax.psum_scatter(term, 'dp', scatter_dimension=0, tiled=True)  22.9 us
    psum x1, waiting for transfers between devices, per_device(): down_coefficient = lax.psum(coeff_part, 'dp')  17.3 us
    reduce_scatter x1, waiting for transfers between devices, per_device(): lax.psum_scatter(contract_trailing(cot_all, down_weight), 'mp', scatter_d...  12.6 us
    dot_general x1, matrix products, per_device(): jnp.einsum('tkf,kdf->td', back_all, gate_up_weight, preferred_element_typ...  11.9 us
  transfers between devices with their start and end apart: 7, of which 7 were waited for; matrix products, arithmetic and copies ran while one was open for 10% of the time, Pallas kernels for 0%

commit v1 on v0

v1 whole, which is shorter than its diff:
```python
import jax
import jax.numpy as jnp
from jax import lax
from jax.experimental import pallas as pl
from jax.experimental.pallas import tpu as pltpu
from jax.sharding import PartitionSpec as P

adapter_scale = 2.0
MESH = pl.DeviceIdType.MESH
F32 = jnp.float32
BF16 = jnp.bfloat16
HIGHEST = lax.Precision.HIGHEST


def dot(left, right, left_dim, right_dim, precision=None):
    return lax.dot_general(
        left,
        right,
        (((left_dim,), (right_dim,)), ((), ())),
        preferred_element_type=F32,
        precision=precision,
    )


def greet(axis, peers):
    barrier = pltpu.get_barrier_semaphore()
    for peer in peers:
        pl.semaphore_signal(barrier, inc=1, device_id={axis: peer}, device_id_type=MESH)
    pl.semaphore_wait(barrier, len(peers))


def remote(axis, peer, source, target, send_sem, recv_sem):
    copy = pltpu.make_async_remote_copy(
        src_ref=source,
        dst_ref=target,
        send_sem=send_sem,
        recv_sem=recv_sem,
        device_id={axis: peer},
        device_id_type=MESH,
    )
    copy.start()
    return copy


def gather_kernel(n, tok_ref, cot_ref, tok_out, cot_out, send_sem, recv_sem):
    me = lax.axis_index("dp")
    rows = tok_ref.shape[0]
    mine = pl.ds(pl.multiple_of(me * rows, rows), rows)
    peers = [lax.rem(me + o, n) for o in range(1, n)]
    greet("dp", peers)
    copies = []
    for a, (source, target) in enumerate(((tok_ref, tok_out), (cot_ref, cot_out))):
        for o, peer in enumerate(peers):
            copies.append(
                remote("dp", peer, source, target.at[mine], send_sem.at[a, o], recv_sem.at[a, o])
            )
    tok_out[mine, :] = tok_ref[...]
    cot_out[mine, :] = cot_ref[...]
    for copy in copies:
        copy.wait()


def middle_kernel(
    n_outer,
    n_inner,
    rows,
    rank,
    small_ref,
    pre_ref,
    back_ref,
    upper_ref,
    down_ref,
    small_out,
    hidden_out,
    grad_out,
    small_in,
    pre_in,
    back_in,
    small_sum,
    pre_sum,
    back_sum,
    small_far,
    pre_far,
    back_far,
    inner_send,
    inner_recv,
    outer_send,
    outer_recv,
    gather_send,
    gather_recv,
    spread_send,
    spread_recv,
):
    me = lax.axis_index("mp")
    outer = me // n_inner
    inner = lax.rem(me, n_inner)

    def place(o, i):
        return lax.rem(outer + o, n_outer) * n_inner + lax.rem(inner + i, n_inner)

    def block(index):
        return pl.ds(pl.multiple_of(index * rows, rows), rows)

    peers = [place(0, i) for i in range(1, n_inner)] + [place(o, 0) for o in range(1, n_outer)]
    greet("mp", peers)

    order = sorted(range(1, n_outer), key=lambda o: -min(o, n_outer - o)) + [0]
    groups = (
        (small_ref, small_in, small_sum, small_far),
        (pre_ref, pre_in, pre_sum, pre_far),
        (back_ref, back_in, back_sum, back_far),
    )

    def part(ref, index):
        return ref.at[:, block(index), :]

    near = {}
    for a, (source, landing, _, _) in enumerate(groups):
        for o in order:
            for i in range(1, n_inner):
                near[a, o, i] = remote(
                    "mp",
                    place(0, i),
                    part(source, place(o, i)),
                    landing.at[i - 1, o],
                    inner_send.at[a, i - 1, o],
                    inner_recv.at[a, i - 1, o],
                )
    far = {}

    def near_total(a, o):
        source, landing, _, _ = groups[a]
        total = source[:, block(place(o, 0)), :].astype(F32)
        for i in range(1, n_inner):
            near[a, o, i].wait_recv()
            total = total + landing[i - 1, o].astype(F32)
        return total

    for a in range(3):
        for o in order[:-1]:
            groups[a][2][o - 1] = near_total(a, o).astype(BF16)
            far[a, o] = remote(
                "mp",
                place(o, 0),
                groups[a][2].at[o - 1],
                groups[a][3].at[o - 1],
                outer_send.at[a, o - 1],
                outer_recv.at[a, o - 1],
            )

    def full_total(a):
        total = near_total(a, 0)
        for o in order[:-1]:
            far[a, o].wait_recv()
            total = total + groups[a][3][o - 1].astype(F32)
        return total

    sent = []
    arrived = {}
    outs = (small_out, hidden_out, grad_out)

    def give(a):
        source = part(outs[a], me)
        for o in order[:-1]:
            arrived[a, o] = remote(
                "mp", place(o, 0), source, source, gather_send.at[a, o - 1], gather_recv.at[a, o - 1]
            )
            sent.append(arrived[a, o])
        spread(a, 0, source)

    def spread(a, o, source):
        for i in range(1, n_inner):
            copy = remote(
                "mp",
                place(0, i),
                source,
                source,
                spread_send.at[a, i - 1, o],
                spread_recv.at[a, i - 1, o],
            )
            sent.append(copy)
            spreads.append(copy)

    spreads = []
    small = full_total(0)[0]
    small_out[0, block(me), :] = small.astype(BF16)
    give(0)
    pre = full_total(1)
    gate = pre[0] + adapter_scale * dot(
        small[:, :rank], upper_ref[0].astype(F32), 1, 0, HIGHEST
    )
    upper = pre[1] + adapter_scale * dot(
        small[:, rank : 2 * rank], upper_ref[1].astype(F32), 1, 0, HIGHEST
    )
    sigma = 1.0 / (1.0 + jnp.exp(-gate))
    hidden_out[0, block(me), :] = (gate * sigma * upper).astype(BF16)
    give(1)
    back_down = small[:, 2 * rank : 3 * rank].astype(BF16)
    hidden_back = full_total(2)[0] + adapter_scale * dot(back_down, down_ref[...], 1, 1)
    grad_out[0, block(me), :] = (
        hidden_back * upper * sigma * (1.0 + gate * (1.0 - sigma))
    ).astype(BF16)
    grad_out[1, block(me), :] = (hidden_back * gate * sigma).astype(BF16)
    give(2)
    for a in range(3):
        for o in order[:-1]:
            arrived[a, o].wait_recv()
            spread(a, o, part(outs[a], place(n_outer - o, 0)))
    for copy in spreads:
        copy.wait_recv()
    for copy in list(near.values()) + list(far.values()) + sent:
        copy.wait_send()


def final_kernel(
    n, rows, out_ref, in_ref, small_ref, out_sum, in_sum, small_sum, out_far, in_far, small_far, send_sem, recv_sem
):
    me = lax.axis_index("dp")

    def block(index):
        return pl.ds(pl.multiple_of(index * rows, rows), rows)

    peers = [lax.rem(me + o, n) for o in range(1, n)]
    greet("dp", peers)
    copies = []
    for o, peer in enumerate(peers):
        copies.append(
            remote("dp", peer, small_ref, small_far.at[o], send_sem.at[0, o], recv_sem.at[0, o])
        )
    for a, (source, landing) in enumerate(((out_ref, out_far), (in_ref, in_far))):
        for o, peer in enumerate(peers):
            copies.append(
                remote(
                    "dp",
                    peer,
                    source.at[block(peer)],
                    landing.at[o],
                    send_sem.at[a + 1, o],
                    recv_sem.at[a + 1, o],
                )
            )
    for copy in copies:
        copy.wait()
    small = small_ref[...].astype(F32)
    total_out = out_ref[block(me), :].astype(F32)
    total_in = in_ref[block(me), :].astype(F32)
    for o in range(n - 1):
        small = small + small_far[o].astype(F32)
        total_out = total_out + out_far[o].astype(F32)
        total_in = total_in + in_far[o].astype(F32)
    small_sum[...] = small
    out_sum[...] = total_out
    in_sum[...] = total_in


def vmem(count):
    return [pl.BlockSpec(memory_space=pltpu.VMEM)] * count


def shape(dims, dtype):
    return jax.ShapeDtypeStruct(dims, dtype)


def communicate(kernel, name, outs, scratch, collective_id, args):
    return pl.pallas_call(
        kernel,
        name=name,
        out_shape=outs,
        in_specs=vmem(len(args)),
        out_specs=vmem(len(outs)),
        scratch_shapes=scratch,
        compiler_params=pltpu.CompilerParams(
            collective_id=collective_id, has_side_effects=True, vmem_limit_bytes=48 * 1024 * 1024
        ),
    )(*args)


def inner_size(n):
    size = 1
    while size * size * 4 <= n:
        size *= 2
    return size


def pad(array):
    width = array.shape[-1]
    extra = -width % 128
    return jnp.pad(array, ((0, 0), (0, extra))) if extra else array


def per_device(
    tokens,
    gate_up_weight,
    down_weight,
    gate_up_input_factor,
    gate_up_output_factor,
    down_input_factor,
    down_output_factor,
    cotangent,
):
    n_dp, n_mp = lax.axis_size("dp"), lax.axis_size("mp")
    tok_rows, width = tokens.shape
    rank, hidden = gate_up_output_factor.shape[1:]
    total = tok_rows * n_dp
    mp_rows = total // n_mp
    gradient_scale = adapter_scale * total ** (-0.5)
    dma = pltpu.SemaphoreType.DMA

    tok, cot = communicate(
        lambda *refs: gather_kernel(n_dp, *refs),
        "gather_rows",
        [shape((total, width), BF16)] * 2,
        [dma((2, n_dp - 1))] * 2,
        0,
        (tokens, cotangent),
    )

    low = jnp.einsum("td,kdr->tkr", tok, gate_up_input_factor, preferred_element_type=F32)
    back_down_part = dot(cot, down_output_factor, 1, 1)
    small = pad(jnp.concatenate([low.reshape(total, 2 * rank), back_down_part], axis=1)).astype(BF16)
    pre = jnp.einsum("td,kdf->ktf", tok, gate_up_weight, preferred_element_type=F32).astype(BF16)
    back = dot(cot, down_weight, 1, 1).astype(BF16)

    n_inner = inner_size(n_mp)
    n_outer = n_mp // n_inner
    small_width = small.shape[1]
    leads, widths = (1, 2, 1), (small_width, hidden, hidden)

    def slots(*count):
        return [pltpu.VMEM((*count, k, mp_rows, w), BF16) for k, w in zip(leads, widths)]

    small_all, hidden_all, grad_all = communicate(
        lambda *refs: middle_kernel(n_outer, n_inner, mp_rows, rank, *refs),
        "middle",
        [
            shape((1, total, small_width), BF16),
            shape((1, total, hidden), BF16),
            shape((2, total, hidden), BF16),
        ],
        [
            *slots(n_inner - 1, n_outer),
            *slots(n_outer - 1),
            *slots(n_outer - 1),
            *[dma((3, n_inner - 1, n_outer))] * 2,
            *[dma((3, n_outer - 1))] * 2,
            *[dma((3, n_outer - 1))] * 2,
            *[dma((3, n_inner - 1, n_outer))] * 2,
        ],
        1,
        (small[None], pre, back[None], gate_up_output_factor, down_input_factor),
    )
    small_all, hidden_all = small_all[0], hidden_all[0]
    back_down = small_all[:, 2 * rank : 3 * rank]

    out_part = dot(hidden_all, down_weight, 1, 0).astype(BF16)
    in_part = jnp.einsum(
        "ktf,kdf->td", grad_all, gate_up_weight, preferred_element_type=F32
    ).astype(BF16)
    low_down_part = dot(hidden_all, down_input_factor, 1, 0)
    back_low_part = [dot(grad_all[k], gate_up_output_factor[k], 1, 1) for k in range(2)]
    small_part = pad(jnp.concatenate([*back_low_part, low_down_part], axis=1)).astype(BF16)

    part_width = small_part.shape[1]
    out_sum, in_sum, small_sum = communicate(
        lambda *refs: final_kernel(n_dp, tok_rows, *refs),
        "final_sums",
        [
            shape((tok_rows, width), F32),
            shape((tok_rows, width), F32),
            shape((total, part_width), F32),
        ],
        [
            pltpu.VMEM((n_dp - 1, tok_rows, width), BF16),
            pltpu.VMEM((n_dp - 1, tok_rows, width), BF16),
            pltpu.VMEM((n_dp - 1, total, part_width), BF16),
            *[dma((3, n_dp - 1))] * 2,
        ],
        2,
        (out_part, in_part, small_part),
    )

    low_all = small_all[:, : 2 * rank].reshape(total, 2, rank)
    upper_gradient = gradient_scale * jnp.stack(
        [dot(low_all[:, k], grad_all[k], 0, 0) for k in range(2)]
    )
    down_input_gradient = gradient_scale * dot(hidden_all, back_down, 0, 0)

    back_low = small_sum[:, : 2 * rank].astype(BF16)
    low_down = small_sum[:, 2 * rank : 3 * rank]
    down_output_gradient = gradient_scale * dot(low_down, cot.astype(F32), 0, 0, HIGHEST)
    lower_gradient = gradient_scale * jnp.stack(
        [dot(tok, back_low[:, k * rank : (k + 1) * rank], 0, 0) for k in range(2)]
    )
    dp_start = lax.axis_index("dp") * tok_rows
    back_low_rows = lax.dynamic_slice_in_dim(back_low, dp_start, tok_rows, 0)
    low_down_rows = lax.dynamic_slice_in_dim(low_down, dp_start, tok_rows, 0)
    output = out_sum + adapter_scale * dot(
        low_down_rows, down_output_factor.astype(F32), 1, 0, HIGHEST
    )
    input_grad = in_sum
    for k in range(2):
        input_grad = input_grad + adapter_scale * dot(
            back_low_rows[:, k * rank : (k + 1) * rank], gate_up_input_factor[k], 1, 1
        )
    return (
        output.astype(BF16),
        input_grad.astype(BF16),
        lower_gradient,
        upper_gradient,
        down_input_gradient,
        down_output_gradient,
    )


def solution(mesh):
    placed = (
        P("dp", "mp"),
        P(None, "mp", "dp"),
        P("dp", "mp"),
        P(None, "mp", None),
        P(None, None, "dp"),
        P("dp", None),
        P(None, "mp"),
        P("dp", "mp"),
    )
    return jax.shard_map(
        per_device,
        mesh=mesh,
        in_specs=placed,
        out_specs=(
            P("dp", "mp"),
            P("dp", "mp"),
            P(None, "mp", None),
            P(None, None, "dp"),
            P("dp", None),
            P(None, "mp"),
        ),
        check_vma=False,
    )
```

time: 429 us -> 165 us (0.38)
  waiting for transfers between devices: 259 us -> 0 us
  Pallas kernels: 0 us -> 111 us
  blocking collectives: 95.9 us -> 0 us
  between operations: 14.2 us -> 0.92 us
  matrix products: 50.8 us -> 41 us
  local copies, waits for them, and re-layouts: 0.84 us -> 7.36 us
  other arithmetic: 6.92 us -> 2.43 us
    reduce_scatter x4 -> x0, waiting for transfers between devices: 131 us -> none  [the longest x1 87.4 us: per_device(): lax.psum_scatter(term, 'mp', scatter_dimension=0, tiled=True)]
    psum x2 -> x0, waiting for transfers between devices: 118 us -> none  [the longest x1 101 us: per_device(): lax.psum(upper_partial, 'mp')]
    pallas_call x0 -> x3, Pallas kernels: none -> 111 us  [communicate(): pl.pallas_call(kernel, name=name, out_shape=outs, in_specs=vmem(len(args)...]
    psum x2 -> x0, blocking collectives: 48.3 us -> none  [the longest x1 37.6 us: per_device(): lax.psum(contract_trailing(cot_all, down_output_factor), 'mp')]
    all_gather x3 -> x0, blocking collectives: 47.6 us -> none  [the longest x1 34.2 us: per_device(): hidden_state_full = lax.all_gather(hidden_state, 'mp', axis=0, tiled=True)]
    dot_general x15 -> x17, matrix products: 50.5 us -> 39.7 us  [the longest x15 20.2 us: dot(): lax.dot_general(left, right, (((left_dim,), (right_dim,)), ((), ())), pre...]
    all_gather x1 -> x0, waiting for transfers between devices: 9.68 us -> none  [per_device(): back_all = lax.all_gather(pre_back, 'mp', axis=0, tiled=True)]
    unnamed x10 -> x23, local copies, waits for them, and re-layouts: 0.84 us -> 6.63 us
  transfers between devices with their start and end apart: 7 -> 0, of which waited for: 7 -> 0; matrix products, arithmetic and copies ran while one was open for 10% -> 0% of each run, Pallas kernels for 0% -> 0%
where the time goes in v1:
time: 165 us; the launch traced here: 163 us
  Pallas kernels  111 us (67%)
  matrix products  41 us (25%)
  local copies, waits for them, and re-layouts  7.36 us (4%)
  other arithmetic  2.43 us (1%)
    pallas_call x3, Pallas kernels, communicate(): pl.pallas_call(kernel, name=name, out_shape=outs, in_specs=vmem(len(args)...  111 us
    dot_general x15, matrix products, dot(): lax.dot_general(left, right, (((left_dim,), (right_dim,)), ((), ())), pre...  20.2 us
    dot_general x1, matrix products, per_device(): jnp.einsum('ktf,kdf->td', grad_all, gate_up_weight, preferred_element_typ...  10.6 us
    dot_general x1, matrix products, per_device(): jnp.einsum('td,kdf->ktf', tok, gate_up_weight, preferred_element_type=F32)  8.98 us
    unnamed x23, local copies, waits for them, and re-layouts  6.63 us

profile of v1, /device:TPU:0, one launch (start us, length us, event | category | flops | bytes accessed | tf_op | source)
XLA Modules:
  0.0 162.9 jit_solution(12623551443396248115)
XLA Ops:
  0.6 0.0 copy-start
  0.6 0.0 copy-start.7
  0.7 0.9 copy-done.7
  1.5 0.0 copy-start.8
  1.5 0.8 copy-done.8
  2.4 9.2 %gather_rows.1 = (bf16[128,1024]{1,0:T(8,128)(2,1)S(1)}, bf16[128,1024]{1,0:T(8,128)(2,1)S(1)}) custom-call(bf16[32,1024]{1,0:T(8,128)(2,1)S(1)} %copy-done.7, bf16[32,1024]{1,0:T(8,128)(2,1)S(1)} %copy-done.8), custom_call_target="tpu_custom_call" | custom-call | tf_op jit(solution)/shard_map/gather_rows/pallas_call | solution.py:265
  11.6 0.0 copy-start.3
  11.6 1.3 fusion.46
  12.9 0.1 copy.27
  13.0 0.0 copy-done
  13.0 0.2 convolution_convert_fusion.6
  13.2 0.1 copy.28
  13.4 9.0 %fusion.refs_1_ = bf16[2,128,3840]{2,1,0:T(8,128)(2,1)} fusion(bf16[2,1024,3840]{2,1,0:T(8,128)(2,1)} %param.9, bf16[128,1024]{1,0:T(8,128)(2,1)S(1)} %get-tuple-element.14), kind=kOutput, calls=%fused_computation.1 | convolution fusion | flops 2014248960 | bytes 17956864 | tf_op jit(solution)/shard_map/td,kdf->ktf/dot_general | solution.py:321
  22.4 0.0 copy-done.3
  22.4 0.0 copy-start.9
  22.4 6.9 %fusion.1.refs_2_ = bf16[1,128,3840]{2,1,0:T(8,128)(2,1)} fusion(bf16[128,1024]{1,0:T(8,128)(2,1)S(1)} %get-tuple-element.15, bf16[3840,1024]{1,0:T(8,128)(2,1)} %param.10), kind=kOutput, calls=%fused_computation.4 | convolution fusion | flops 1007124480 | bytes 9109504 | tf_op jit(solution)/shard_map/dot_general | solution.py:16
  29.3 0.0 copy-done.9
  29.3 1.3 copy.29.refs_4_
  30.6 0.0 copy-start.1
  30.6 1.2 copy-done.1
  31.8 0.0 copy-start.2
  31.8 1.2 copy-done.2
  33.0 0.0 copy-start.5
  33.0 1.2 copy-done.5
  34.2 91.1 %middle.1 = (bf16[1,128,256]{2,1,0:T(8,128)(2,1)S(1)}, bf16[1,128,3840]{2,1,0:T(8,128)(2,1)S(1)}, bf16[2,128,3840]{2,1,0:T(8,128)(2,1)S(1)}) custom-call(bf16[1,128,256]{2,1,0:T(8,128)(2,1)S(1)} %fusion.34.refs_0_, bf16[2,128,3840]{2,1,0:T(8,128)(2,1)} %fusion.refs_1_, bf16[1,128,3840]{2,1,0:T(8,128)(2,1)S(1)} %copy-done.1, ...), custom_call_target="tpu_custom_call" | custom-call | tf_op jit(solution)/shard_map/middle/pallas_call | solution.py:265
  125.3 0.1 copy.33
  125.4 0.3 convolution_bitcast_fusion.1
  125.7 0.3 convolution_bitcast_fusion
  126.0 0.0 copy-start.6
  126.0 1.4 maximum_multiply_fusion
  127.5 0.0 copy-done.6
  127.5 0.4 convolution_convert_fusion.5
  127.9 0.1 copy.30
  128.1 1.5 convolution_convert_fusion.4
  129.6 0.1 copy.31
  129.7 1.5 convolution_convert_fusion.3
  131.2 0.1 copy.32
  131.3 0.1 fusion.36.refs_2_
  131.4 10.6 %fusion.2.refs_1_ = bf16[128,1024]{1,0:T(8,128)(2,1)S(1)} fusion(bf16[2,128,3840]{2,1,0:T(8,128)(2,1)S(1)} %get-tuple-element.17, bf16[2,1024,3840]{2,1,0:T(8,128)(2,1)} %param.9), kind=kOutput, calls=%fused_computation.9 | convolution fusion | flops 2013396992 | bytes 17956864 | tf_op jit(solution)/shard_map/ktf,kdf->td/dot_general | solution.py:356
  142.0 4.4 %convolution_convert_fusion.2.refs_0_ = bf16[128,1024]{1,0:T(8,128)(2,1)S(1)} fusion(bf16[3840,1024]{1,0:T(8,128)(2,1)} %param.10, bf16[1,128,3840]{2,1,0:T(8,128)(2,1)S(1)} %get-tuple-element.16), kind=kOutput, calls=%fused_computation.10 | convolution fusion | flops 1006764032 | bytes 9109504 | tf_op jit(solution)/shard_map/dot_general | solution.py:16
  146.4 0.0 copy-start.4
  146.4 0.0 copy-start.10
  146.4 10.9 %final_sums.1 = (f32[32,1024]{1,0:T(8,128)S(1)}, f32[32,1024]{1,0:T(8,128)S(1)}, f32[128,256]{1,0:T(8,128)S(1)}) custom-call(bf16[128,1024]{1,0:T(8,128)(2,1)S(1)} %convolution_convert_fusion.2.refs_0_, bf16[128,1024]{1,0:T(8,128)(2,1)S(1)} %fusion.2.refs_1_, bf16[128,256]{1,0:T(8,128)(2,1)S(1)} %fusion.36.refs_2_), custom_call_target="tpu_custom_call" | custom-call | tf_op jit(solution)/shard_map/final_sums/pallas_call | solution.py:265
  157.3 0.2 convolution_bitcast_fusion.4
  157.6 0.3 convolution_bitcast_fusion.3
  157.9 0.8 maximum_multiply_fusion.1
  158.7 0.0 copy-done.4
  158.7 1.0 convolution_multiply_fusion.1
  159.7 0.0 copy-done.10
  159.7 0.2 convolution_multiply_fusion.2
  160.0 0.8 fusion.6
  160.8 0.8 fusion.7
  161.6 1.3 convolution_multiply_fusion
  (6 shorter events, 0.1 us)
Async XLA Ops:
  0.6 12.4 %copy-start = (bf16[64,1024]{1,0:T(8,128)(2,1)S(1)}, bf16[64,1024]{1,0:T(8,128)(2,1)}, u32[]{:S(2)}) copy-start(bf16[64,1024]{1,0:T(8,128)(2,1)} %param.14) | copy-start | bytes 393220
  0.6 0.9 copy-start.7
  1.5 0.8 copy-start.8
  11.6 10.8 %copy-start.3 = (bf16[128,1024]{1,0:T(8,128)(2,1)}, bf16[128,1024]{1,0:T(8,128)(2,1)S(1)}, u32[]{:S(2)}) copy-start(bf16[128,1024]{1,0:T(8,128)(2,1)S(1)} %get-tuple-element.15) | copy-start | bytes 786436
  22.4 6.9 %copy-start.9 = (bf16[3840,64]{0,1:T(8,128)(2,1)S(1)}, bf16[3840,64]{0,1:T(8,128)(2,1)}, u32[]{:S(2)}) copy-start(bf16[3840,64]{0,1:T(8,128)(2,1)} %param.13) | copy-start | bytes 1474564
  30.6 1.2 copy-start.1
  31.8 1.2 copy-start.2
  33.0 1.2 copy-start.5
  126.0 1.5 copy-start.6
  146.4 12.3 %copy-start.4 = (bf16[128,1024]{1,0:T(8,128)(2,1)S(1)}, bf16[128,1024]{1,0:T(8,128)(2,1)}, u32[]{:S(2)}) copy-start(bf16[128,1024]{1,0:T(8,128)(2,1)} %copy-done.3) | copy-start | bytes 786436
  146.4 13.3 %copy-start.10 = (bf16[2,1024,64]{1,2,0:T(8,128)(2,1)S(1)}, bf16[2,1024,64]{1,2,0:T(8,128)(2,1)}, u32[]{:S(2)}) copy-start(bf16[2,1024,64]{1,2,0:T(8,128)(2,1)} %param.11) | copy-start | bytes 786436

commit v2 on v1

v2 whole, which is shorter than its diff:
```python
import jax
import jax.numpy as jnp
from jax import lax
from jax.experimental import pallas as pl
from jax.experimental.pallas import tpu as pltpu
from jax.sharding import PartitionSpec as P

adapter_scale = 2.0
MESH = pl.DeviceIdType.MESH
F32 = jnp.float32
BF16 = jnp.bfloat16
HIGHEST = lax.Precision.HIGHEST


def dot(left, right, left_dim, right_dim, precision=None):
    return lax.dot_general(
        left,
        right,
        (((left_dim,), (right_dim,)), ((), ())),
        preferred_element_type=F32,
        precision=precision,
    )


def remote(axis, peer, source, target, send_sem, recv_sem):
    copy = pltpu.make_async_remote_copy(
        src_ref=source,
        dst_ref=target,
        send_sem=send_sem,
        recv_sem=recv_sem,
        device_id={axis: peer},
        device_id_type=MESH,
    )
    copy.start()
    return copy


def tile_of(size):
    return max(t for t in range(128, 1281, 128) if size % t == 0)


def layer_kernel(
    n_dp,
    n_outer,
    n_inner,
    rank,
    tok_ref,
    cot_ref,
    lower_ref,
    upper_ref,
    down_in_ref,
    down_out_ref,
    weight_hbm,
    down_hbm,
    tok_out,
    cot_out,
    small_out,
    hidden_out,
    grad_out,
    out_sum,
    in_sum,
    low_sum,
    weight,
    down,
    small_part,
    gate_part,
    up_part,
    back_part,
    wide_in,
    wide_sum,
    wide_far,
    small_in,
    small_mid,
    small_far,
    total_acc,
    out_part,
    in_part,
    low_part,
    out_far,
    in_far,
    low_far,
    load_sem,
    first_send,
    first_recv,
    inner_send,
    inner_recv,
    outer_send,
    outer_recv,
    gather_send,
    gather_recv,
    spread_send,
    spread_recv,
    last_send,
    last_recv,
):
    me_dp = lax.axis_index("dp")
    me = lax.axis_index("mp")
    outer = me // n_inner
    inner = lax.rem(me, n_inner)
    tok_rows = tok_ref.shape[0]
    total = tok_out.shape[0]
    rows = total // (n_outer * n_inner)
    hidden_size = down.shape[0]
    tile = tile_of(hidden_size)
    tiles = hidden_size // tile

    loads = [
        pltpu.make_async_copy(weight_hbm.at[0], weight.at[0], load_sem.at[0]),
        pltpu.make_async_copy(weight_hbm.at[1], weight.at[1], load_sem.at[1]),
        pltpu.make_async_copy(down_hbm, down, load_sem.at[2]),
    ]
    for load in loads:
        load.start()

    def place(o, i):
        return lax.rem(outer + o, n_outer) * n_inner + lax.rem(inner + i, n_inner)

    def block(index, size=rows):
        return pl.ds(pl.multiple_of(index * size, size), size)

    dp_peers = [lax.rem(me_dp + o, n_dp) for o in range(1, n_dp)]
    mp_peers = [place(0, i) for i in range(1, n_inner)] + [place(o, 0) for o in range(1, n_outer)]
    barrier = pltpu.get_barrier_semaphore()
    for axis, peers in (("dp", dp_peers), ("mp", mp_peers)):
        for peer in peers:
            pl.semaphore_signal(barrier, inc=1, device_id={axis: peer}, device_id_type=MESH)
    pl.semaphore_wait(barrier, len(dp_peers) + len(mp_peers))

    mine = block(me_dp, tok_rows)
    sent = []
    first = []
    for a, (source, target) in enumerate(((tok_ref, tok_out), (cot_ref, cot_out))):
        for o, peer in enumerate(dp_peers):
            first.append(
                remote("dp", peer, source, target.at[mine], first_send.at[a, o], first_recv.at[a, o])
            )
    sent += first
    tok_out[mine, :] = tok_ref[...]
    cot_out[mine, :] = cot_ref[...]

    order = sorted(range(1, n_outer), key=lambda o: -min(o, n_outer - o)) + [0]
    sources = (small_part, gate_part, up_part, back_part)

    def landing(a, *index):
        return small_in.at[index] if a == 0 else wide_in.at[(a - 1, *index)]

    def middle(a, o):
        return small_mid.at[o] if a == 0 else wide_sum.at[a - 1, o]

    def distant(a, o):
        return small_far.at[o] if a == 0 else wide_far.at[a - 1, o]

    near = {}

    def send_near(a):
        for o in order:
            for i in range(1, n_inner):
                near[a, o, i] = remote(
                    "mp",
                    place(0, i),
                    sources[a].at[block(place(o, i))],
                    landing(a, i - 1, o),
                    inner_send.at[a, i - 1, o],
                    inner_recv.at[a, i - 1, o],
                )
                sent.append(near[a, o, i])

    def columns(t):
        return pl.ds(pl.multiple_of(t * tile, tile), tile)

    for copy in first[: n_dp - 1]:
        copy.wait_recv()
    loads[0].wait()

    @pl.loop(0, tiles)
    def _(t):
        gate_part[:, columns(t)] = dot(tok_out[...], weight[0, :, columns(t)], 1, 0).astype(BF16)

    send_near(1)
    loads[1].wait()

    @pl.loop(0, tiles)
    def _(t):
        up_part[:, columns(t)] = dot(tok_out[...], weight[1, :, columns(t)], 1, 0).astype(BF16)

    for copy in first[n_dp - 1 :]:
        copy.wait_recv()
    pieces = [dot(tok_out[...], lower_ref[k], 1, 0) for k in range(2)]
    pieces.append(dot(cot_out[...], down_out_ref[...], 1, 1))
    pieces.append(jnp.zeros_like(pieces[0]))
    small_part[...] = jnp.concatenate(pieces, axis=1).astype(BF16)
    send_near(0)
    send_near(2)
    loads[2].wait()

    @pl.loop(0, tiles)
    def _(t):
        back_part[:, columns(t)] = dot(cot_out[...], down[columns(t), :], 1, 1).astype(BF16)

    send_near(3)
    far = {}

    def near_total(a, o):
        summed = sources[a][block(place(o, 0)), :].astype(F32)
        for i in range(1, n_inner):
            near[a, o, i].wait_recv()
            summed = summed + landing(a, i - 1, o)[...].astype(F32)
        return summed

    for a in (1, 0, 2, 3):
        for o in order[:-1]:
            middle(a, o - 1)[...] = near_total(a, o).astype(BF16)
            far[a, o] = remote(
                "mp",
                place(o, 0),
                middle(a, o - 1),
                distant(a, o - 1),
                outer_send.at[a, o - 1],
                outer_recv.at[a, o - 1],
            )
            sent.append(far[a, o])

    def full_total(a):
        summed = near_total(a, 0)
        for o in order[:-1]:
            far[a, o].wait_recv()
            summed = summed + distant(a, o - 1)[...].astype(F32)
        return summed

    arrived = {}
    spreads = {}
    outs = (small_out, hidden_out, grad_out.at[0], grad_out.at[1])

    def spread_block(a, o, source):
        for i in range(1, n_inner):
            spreads[a, o, i] = remote(
                "mp",
                place(0, i),
                source,
                source,
                spread_send.at[a, i - 1, o],
                spread_recv.at[a, i - 1, o],
            )
            sent.append(spreads[a, o, i])

    def give(a):
        source = outs[a].at[block(me)]
        for o in order[:-1]:
            arrived[a, o] = remote(
                "mp", place(o, 0), source, source, gather_send.at[a, o - 1], gather_recv.at[a, o - 1]
            )
            sent.append(arrived[a, o])
        spread_block(a, 0, source)

    def spread(a):
        for o in order[:-1]:
            arrived[a, o].wait_recv()
            spread_block(a, o, outs[a].at[block(place(n_outer - o, 0))])

    def complete(a):
        for o in order:
            for i in range(1, n_inner):
                spreads[a, o, i].wait_recv()

    gate = full_total(1)
    small = full_total(0)
    small_out[block(me), :] = small.astype(BF16)
    give(0)
    gate = gate + adapter_scale * dot(small[:, :rank], upper_ref[0].astype(F32), 1, 0, HIGHEST)
    sigma = 1.0 / (1.0 + jnp.exp(-gate))
    upper = full_total(2) + adapter_scale * dot(
        small[:, rank : 2 * rank], upper_ref[1].astype(F32), 1, 0, HIGHEST
    )
    hidden_out[block(me), :] = (gate * sigma * upper).astype(BF16)
    give(1)
    back_down = small[:, 2 * rank : 3 * rank].astype(BF16)
    back_adapter = adapter_scale * dot(back_down, down_in_ref[...], 1, 1)
    hidden_back = full_total(3) + back_adapter
    grad_out[0, block(me), :] = (
        hidden_back * upper * sigma * (1.0 + gate * (1.0 - sigma))
    ).astype(BF16)
    give(2)
    grad_out[1, block(me), :] = (hidden_back * gate * sigma).astype(BF16)
    give(3)
    spread(0)
    spread(1)
    spread(2)

    last = []

    def send_last(a, source, landing_ref):
        for o, peer in enumerate(dp_peers):
            cut = source if a == 0 else source.at[block(peer, tok_rows)]
            last.append(
                remote("dp", peer, cut, landing_ref.at[o], last_send.at[a, o], last_recv.at[a, o])
            )

    complete(0)
    complete(1)
    total_acc[...] = jnp.zeros_like(total_acc)

    @pl.loop(0, tiles)
    def _(t):
        total_acc[...] += dot(hidden_out[:, columns(t)], down[columns(t), :], 1, 0)

    out_part[...] = total_acc[...].astype(BF16)
    send_last(1, out_part, out_far)
    low_down = dot(hidden_out[...], down_in_ref[...], 1, 0)
    total_acc[...] = jnp.zeros_like(total_acc)
    spread(3)
    back_lows = []
    for k in range(2):
        complete(2 + k)

        @pl.loop(0, tiles)
        def _(t):
            total_acc[...] += dot(grad_out[k, :, columns(t)], weight[k, :, columns(t)], 1, 1)

        back_lows.append(dot(grad_out[k], upper_ref[k], 1, 1))
    low_part[...] = jnp.concatenate(
        [*back_lows, low_down, jnp.zeros_like(low_down)], axis=1
    ).astype(BF16)
    in_part[...] = total_acc[...].astype(BF16)
    send_last(0, low_part, low_far)
    send_last(2, in_part, in_far)

    for copy in last:
        copy.wait_recv()
    low_total = low_part[...].astype(F32)
    total_out = out_part[mine, :].astype(F32)
    total_in = in_part[mine, :].astype(F32)
    for o in range(n_dp - 1):
        low_total = low_total + low_far[o].astype(F32)
        total_out = total_out + out_far[o].astype(F32)
        total_in = total_in + in_far[o].astype(F32)
    low_sum[...] = low_total
    out_sum[...] = total_out
    in_sum[...] = total_in
    for copy in sent + last:
        copy.wait_send()


def shape(dims, dtype):
    return jax.ShapeDtypeStruct(dims, dtype)


def inner_size(n):
    size = 1
    while size * size * 4 <= n:
        size *= 2
    return size


def per_device(
    tokens,
    gate_up_weight,
    down_weight,
    gate_up_input_factor,
    gate_up_output_factor,
    down_input_factor,
    down_output_factor,
    cotangent,
):
    n_dp, n_mp = lax.axis_size("dp"), lax.axis_size("mp")
    tok_rows, width = tokens.shape
    rank, hidden = gate_up_output_factor.shape[1:]
    total = tok_rows * n_dp
    mp_rows = total // n_mp
    gradient_scale = adapter_scale * total ** (-0.5)
    dma = pltpu.SemaphoreType.DMA

    n_inner = inner_size(n_mp)
    n_outer = n_mp // n_inner
    small_width = 4 * rank
    vmem = pl.BlockSpec(memory_space=pltpu.VMEM)
    hbm = pl.BlockSpec(memory_space=pltpu.HBM)

    def buffer(*dims, dtype=BF16):
        return pltpu.VMEM(dims, dtype)

    tok, cot, small_all, hidden_all, grad_all, out_sum, in_sum, small_sum = pl.pallas_call(
        lambda *refs: layer_kernel(n_dp, n_outer, n_inner, rank, *refs),
        name="layer",
        out_shape=[
            shape((total, width), BF16),
            shape((total, width), BF16),
            shape((total, small_width), BF16),
            shape((total, hidden), BF16),
            shape((2, total, hidden), BF16),
            shape((tok_rows, width), F32),
            shape((tok_rows, width), F32),
            shape((total, small_width), F32),
        ],
        in_specs=[vmem] * 6 + [hbm] * 2,
        out_specs=[vmem] * 8,
        scratch_shapes=[
            buffer(2, width, hidden),
            buffer(hidden, width),
            buffer(total, small_width),
            buffer(total, hidden),
            buffer(total, hidden),
            buffer(total, hidden),
            buffer(3, n_inner - 1, n_outer, mp_rows, hidden),
            buffer(3, n_outer - 1, mp_rows, hidden),
            buffer(3, n_outer - 1, mp_rows, hidden),
            buffer(n_inner - 1, n_outer, mp_rows, small_width),
            buffer(n_outer - 1, mp_rows, small_width),
            buffer(n_outer - 1, mp_rows, small_width),
            buffer(total, width, dtype=F32),
            buffer(total, width),
            buffer(total, width),
            buffer(total, small_width),
            buffer(n_dp - 1, tok_rows, width),
            buffer(n_dp - 1, tok_rows, width),
            buffer(n_dp - 1, total, small_width),
            dma((3,)),
            *[dma((2, n_dp - 1))] * 2,
            *[dma((4, n_inner - 1, n_outer))] * 2,
            *[dma((4, n_outer - 1))] * 2,
            *[dma((4, n_outer - 1))] * 2,
            *[dma((4, n_inner - 1, n_outer))] * 2,
            *[dma((3, n_dp - 1))] * 2,
        ],
        compiler_params=pltpu.CompilerParams(
            collective_id=0, has_side_effects=True, vmem_limit_bytes=56 * 1024 * 1024
        ),
    )(
        tokens,
        cotangent,
        gate_up_input_factor,
        gate_up_output_factor,
        down_input_factor,
        down_output_factor,
        gate_up_weight,
        down_weight,
    )
    back_down = small_all[:, 2 * rank : 3 * rank]

    low_all = small_all[:, : 2 * rank].reshape(total, 2, rank)
    upper_gradient = gradient_scale * jnp.stack(
        [dot(low_all[:, k], grad_all[k], 0, 0) for k in range(2)]
    )
    down_input_gradient = gradient_scale * dot(hidden_all, back_down, 0, 0)

    back_low = small_sum[:, : 2 * rank].astype(BF16)
    low_down = small_sum[:, 2 * rank : 3 * rank]
    down_output_gradient = gradient_scale * dot(low_down, cot.astype(F32), 0, 0, HIGHEST)
    lower_gradient = gradient_scale * jnp.stack(
        [dot(tok, back_low[:, k * rank : (k + 1) * rank], 0, 0) for k in range(2)]
    )
    dp_start = lax.axis_index("dp") * tok_rows
    back_low_rows = lax.dynamic_slice_in_dim(back_low, dp_start, tok_rows, 0)
    low_down_rows = lax.dynamic_slice_in_dim(low_down, dp_start, tok_rows, 0)
    output = out_sum + adapter_scale * dot(
        low_down_rows, down_output_factor.astype(F32), 1, 0, HIGHEST
    )
    input_grad = in_sum
    for k in range(2):
        input_grad = input_grad + adapter_scale * dot(
            back_low_rows[:, k * rank : (k + 1) * rank], gate_up_input_factor[k], 1, 1
        )
    return (
        output.astype(BF16),
        input_grad.astype(BF16),
        lower_gradient,
        upper_gradient,
        down_input_gradient,
        down_output_gradient,
    )


def solution(mesh):
    placed = (
        P("dp", "mp"),
        P(None, "mp", "dp"),
        P("dp", "mp"),
        P(None, "mp", None),
        P(None, None, "dp"),
        P("dp", None),
        P(None, "mp"),
        P("dp", "mp"),
    )
    return jax.shard_map(
        per_device,
        mesh=mesh,
        in_specs=placed,
        out_specs=(
            P("dp", "mp"),
            P("dp", "mp"),
            P(None, "mp", None),
            P(None, None, "dp"),
            P("dp", None),
            P(None, "mp"),
        ),
        check_vma=False,
    )
```

time: 165 us -> 124 us (0.75)
  matrix products: 41 us -> 6.47 us
  Pallas kernels: 111 us -> 107 us
  local copies, waits for them, and re-layouts: 7.36 us -> 5.27 us
    dot_general x2 -> x0, matrix products: 19.5 us -> none  [the longest x1 10.6 us: per_device(): jnp.einsum('ktf,kdf->td', grad_all, gate_up_weight, preferred_element_typ...]
    dot_general x15 -> x9, matrix products: 20.2 us -> 6.47 us  [dot(): lax.dot_general(left, right, (((left_dim,), (right_dim,)), ((), ())), pre...]
    pallas_call x3 -> x1, Pallas kernels: 111 us -> 107 us  [per_device(): pl.pallas_call(lambda *refs: layer_kernel(n_dp, n_outer, n_inner, rank, *...]
    unnamed x23 -> x18, local copies, waits for them, and re-layouts: 6.63 us -> 4.31 us
where the time goes in v2:
time: 124 us; the launch traced here: 122 us
  Pallas kernels  107 us (86%)
  matrix products  6.47 us (5%)
  local copies, waits for them, and re-layouts  5.27 us (4%)
  other arithmetic  2.3 us (2%)
    pallas_call x1, Pallas kernels, per_device(): pl.pallas_call(lambda *refs: layer_kernel(n_dp, n_outer, n_inner, rank, *...  107 us
    dot_general x9, matrix products, dot(): lax.dot_general(left, right, (((left_dim,), (right_dim,)), ((), ())), pre...  6.47 us
    unnamed x18, local copies, waits for them, and re-layouts  4.31 us

profile of v2, /device:TPU:0, one launch (start us, length us, event | category | flops | bytes accessed | tf_op | source)
XLA Modules:
  0.0 121.9 jit_solution(7086195251219856625)
XLA Ops:
  0.6 2.0 %copy.16.refs_2_ = bf16[2,1024,64]{2,1,0:T(8,128)(2,1)} copy(bf16[2,1024,64]{1,2,0:T(8,128)(2,1)} %param.11) | data formatting | bytes 524288 | tf_op args[3]
  2.6 2.3 %copy.17.refs_4_ = bf16[3840,64]{1,0:T(8,128)(2,1)} copy(bf16[3840,64]{0,1:T(8,128)(2,1)} %param.13) | data formatting | bytes 983040 | tf_op args[5]
  4.9 107.1 %layer.1 = (bf16[128,1024]{1,0:T(8,128)(2,1)}, bf16[128,1024]{1,0:T(8,128)(2,1)}, bf16[128,256]{1,0:T(8,128)(2,1)}, bf16[128,3840]{1,0:T(8,128)(2,1)}, bf16[2,12...) custom-call(bf16[32,1024]{1,0:T(8,128)(2,1)} %refs_0_.1, ...), custom_call_target="tpu_custom_call" | custom-call | tf_op jit(solution)/shard_map/layer/pallas_call | solution.py:381
  112.0 0.0 copy-start.4
  112.0 0.0 copy-start.5
  112.0 0.0 copy-start.3
  112.1 0.0 copy-start.7
  112.1 0.0 copy-start.1
  112.1 0.0 copy-start.6
  112.1 0.8 slice.53
  112.9 0.0 copy-start.2
  112.9 2.5 %convolution_multiply_fusion = f32[3840,64]{0,1:T(8,128)} fusion(bf16[128,3840]{1,0:T(8,128)(2,1)} %get-tuple-element.20, bf16[128,256]{1,0:T(8,128)(2,1)} %get-tuple-element.18), kind=kOutput, calls=%fused_computation | convolution fusion | flops 63160320 | bytes 1998848 | tf_op jit(solution)/shard_map/dot_general | solution.py:16
  115.5 0.1 copy.18
  115.6 0.0 copy-done.4
  115.6 0.0 copy-start
  115.7 0.0 copy-done.5
  115.7 1.0 convolution_multiply_fusion.1
  116.7 0.0 copy-done.3
  116.7 0.0 copy-done.7
  116.7 0.8 fusion.4
  117.5 0.0 copy-done.1
  117.5 0.2 convolution_multiply_fusion.2
  117.7 0.0 copy-done.6
  117.7 0.8 fusion.3
  118.5 0.0 copy-done.2
  118.5 0.3 convolution_bitcast_fusion.2
  118.8 0.2 convolution_bitcast_fusion.3
  119.1 0.8 maximum_multiply_fusion.1
  119.9 0.0 copy-done
  119.9 0.3 convolution_bitcast_fusion
  120.2 0.3 convolution_bitcast_fusion.1
  120.5 1.4 %maximum_multiply_fusion = f32[2,64,3840]{2,1,0:T(8,128)} fusion(f32[1,64,3840]{2,1,0:T(8,128)S(1)} %convolution_bitcast_fusion, f32[1,64,3840]{2,1,0:T(8,128)S(1)} %convolution_bitcast_fusion.1), kind=kLoop, calls=%fused_computation.3 | loop fusion | flops 983040 | bytes 3932160 | tf_op jit(solution)/shard_map/mul | solution.py:440
  (3 shorter events, 0.0 us)
Async XLA Ops:
  112.0 3.6 %copy-start.4 = (f32[128,256]{1,0:T(8,128)S(1)}, f32[128,256]{1,0:T(8,128)}, u32[]{:S(2)}) copy-start(f32[128,256]{1,0:T(8,128)} %get-tuple-element.15) | copy-start | bytes 393220
  112.0 3.6 %copy-start.5 = (bf16[128,1024]{1,0:T(8,128)(2,1)S(1)}, bf16[128,1024]{1,0:T(8,128)(2,1)}, u32[]{:S(2)}) copy-start(bf16[128,1024]{1,0:T(8,128)(2,1)} %get-tuple-element.21) | copy-start | bytes 786436
  112.0 4.6 %copy-start.3 = (bf16[64,1024]{1,0:T(8,128)(2,1)S(1)}, bf16[64,1024]{1,0:T(8,128)(2,1)}, u32[]{:S(2)}) copy-start(bf16[64,1024]{1,0:T(8,128)(2,1)} %refs_5_.1) | copy-start | bytes 393220
  112.1 4.6 %copy-start.7 = (f32[32,1024]{1,0:T(8,128)S(1)}, f32[32,1024]{1,0:T(8,128)}, u32[]{:S(2)}) copy-start(f32[32,1024]{1,0:T(8,128)} %get-tuple-element.14) | copy-start | bytes 393220
  112.1 5.5 %copy-start.1 = (bf16[2,1024,64]{1,2,0:T(8,128)(2,1)S(1)}, bf16[2,1024,64]{1,2,0:T(8,128)(2,1)}, u32[]{:S(2)}) copy-start(bf16[2,1024,64]{1,2,0:T(8,128)(2,1)} %param.11) | copy-start | bytes 786436
  112.1 5.7 %copy-start.6 = (f32[32,1024]{1,0:T(8,128)S(1)}, f32[32,1024]{1,0:T(8,128)}, u32[]{:S(2)}) copy-start(f32[32,1024]{1,0:T(8,128)} %get-tuple-element.16) | copy-start | bytes 393220
  112.9 5.6 %copy-start.2 = (bf16[128,1024]{1,0:T(8,128)(2,1)S(1)}, bf16[128,1024]{1,0:T(8,128)(2,1)}, u32[]{:S(2)}) copy-start(bf16[128,1024]{1,0:T(8,128)(2,1)} %get-tuple-element.17) | copy-start | bytes 786436
  115.6 4.3 %copy-start = (bf16[2,128,3840]{2,1,0:T(8,128)(2,1)S(1)}, bf16[2,128,3840]{2,1,0:T(8,128)(2,1)}, u32[]{:S(2)}) copy-start(bf16[2,128,3840]{2,1,0:T(8,128)(2,1)} %get-tuple-element.19) | copy-start | bytes 5898244
